TPU v7x, 256 devices: a whole 4x4x8 slice. The times are simulated.
256 devices in a mesh: chan: 64 (over x, y, z_hi, core), tm: 4 (over z_lo).
Axes of the slice: x: 4, y: 4, z: 8 (z_hi: 2, z_lo: 4; z = z_hi * 4 + z_lo), core: 2. Of those that a mesh axis runs over, the one named last changes fastest.
Arguments:
- voltages: bfloat16 [2, 64, 2048, 512], P(None, None, 'chan', 'tm'), may hold values from -0.25 to 0.25
- assignment: int32 [1024, 1], replicated, may hold values from 0 to 7; in each aligned block of 1024 rows (0 to 1023, 1024 to 2047, ...) at most 192 rows name the same one
- slot_subarray_index: int32 [8], replicated, may hold values from 0 to 7, each once
Outputs:
- visibilities: float32 [8, 64, 2, 384, 384], P('tm', 'chan')
Inputs may be any that keep to these rules, and one draw needn't show every extreme that they name: `assignment`: no subarray holds more than 192 antennas; one holds exactly 192. `slot_subarray_index`: each subarray appears once.
All inputs are finite; a program needn't handle non-finite values.
Results may differ from a plain program's by a relative error of at most 0.008.
Values may be sent and summed in bfloat16 or wider, within the bound.
A program may use at most 64 MiB of HBM per device.

v0:
```python
import functools

import jax
import jax.numpy as jnp
from jax import lax
from jax.experimental import pallas as pl
from jax.experimental.pallas import tpu as pltpu
from jax.sharding import PartitionSpec as P

SLOT = 384
LEVELS = (288, 304, 320, 336, 352, 368, 384, 400, 432, 768)
PEERS = 32
BF = jnp.bfloat16
MESH = pl.DeviceIdType.MESH
NT = (((1,), (1,)), ((), ()))
VMEM = pl.BlockSpec(memory_space=pltpu.VMEM)
SMEM = pl.BlockSpec(memory_space=pltpu.SMEM)
ANY = pl.BlockSpec(memory_space=pl.ANY)


def div(a, b):
    return lax.div(a, jnp.int32(b))


def rem(a, b):
    return lax.rem(a, jnp.int32(b))


def count_dot(a, b):
    return jnp.dot(as_bf16(a), as_bf16(b), preferred_element_type=jnp.float32)


def as_bf16(values):
    return values.astype(jnp.float32).astype(BF)


def iota(shape, dim):
    return lax.broadcasted_iota(jnp.int32, shape, dim)


def slots_of(assigned, index_ref):
    slot = jnp.zeros_like(assigned)
    for s in range(8):
        slot = jnp.where(assigned == index_ref[s], s, slot)
    return slot


def level_kernel(assigned_ref, index_ref, level_ref):
    pair = slots_of(assigned_ref[...], index_ref) >> 1
    half = (iota((8, 128), 1) >> 5) & 1
    most = jnp.int32(0)
    for g in range(4):
        for h in range(2):
            most = jnp.maximum(most, jnp.sum(jnp.where((pair == g) & (half == h), 2, 0)))
    level = jnp.int32(0)
    for rows in LEVELS[:-1]:
        level = level + jnp.where(most > rows, 1, 0)
    level_ref[0] = level


def counts_before(masks, same, before):
    n = len(masks)
    found = count_dot(jnp.concatenate(masks, axis=0), jnp.concatenate([same & before, same], axis=1))
    sub, other = iota((8 * n, 8 * n), 0), iota((8 * n, 8 * n), 1)
    earlier = ((sub >> 3) == (other >> 3)) & (sub > other)
    total = (found[:, :128] + count_dot(earlier, found[:, 128:])).astype(jnp.int32)
    return [total[8 * i : 8 * i + 8] for i in range(n)]


def to_rows(values, half):
    source, target = iota((128, 128), 0), iota((128, 128), 1)
    pick = source == (target >> 6) * 64 + half * 32 + ((target & 63) >> 1)
    moved = count_dot(jnp.concatenate(values, axis=0), pick).astype(jnp.int32)
    return [moved[8 * i : 8 * i + 8] for i in range(len(values))]


def correlate(
    K, assigned_hbm, index_hbm, v_ref, z, assigned_ref, index_ref, v, buf, select, merge, stage, recv, notes,
    in_sem, send1, recv1, send2, recv2,
):
    chan, t = lax.axis_index("chan"), lax.axis_index("tm")
    xy, h, core = div(chan, 4), rem(div(chan, 2), 2), rem(chan, 2)
    me, depth = xy * 2 + core, h * 4 + t

    x, y = div(xy, 4), rem(xy, 4)

    def group(four, i):
        there = rem(x + 3 - div(four, 2), 4) * 4 + rem(y + 3 - 2 * rem(four, 2) - i // 2, 4)
        there_core = rem(core + 1 - i % 2, 2)
        return there, there_core, {"chan": (there * 2 + h) * 2 + there_core, "tm": t}

    def others(act):
        def step(four, carry):
            for i in range(4):
                act(*group(four, i))
            return carry

        lax.fori_loop(0, PEERS // 4 - 1, step, 0)
        for i in range(3):
            act(*group(jnp.int32(PEERS // 4 - 1), i))

    def column(half, row):
        return {"chan": (xy * 2 + half) * 2 + core, "tm": row}

    loads = [
        pltpu.make_async_copy(source, target, in_sem.at[n])
        for n, (source, target) in enumerate(((assigned_hbm, assigned_ref), (index_hbm, index_ref), (v_ref, v)))
    ]
    for load in loads:
        load.start()
    barrier = pltpu.get_barrier_semaphore()

    for o in (4, 5, 7, 6, 1, 2, 3):
        pl.semaphore_signal(
            barrier, inc=1, device_id=column(rem(h + o // 4, 2), rem(t + o, 4)), device_id_type=MESH
        )
    others(lambda there, there_core, device: pl.semaphore_signal(
        barrier, inc=1, device_id=device, device_id_type=MESH
    ))

    loads[0].wait()
    loads[1].wait()
    slot = slots_of(assigned_ref[...], index_ref)
    pair = slot >> 1
    source, target = iota((128, 128), 0), iota((128, 128), 1)
    same, before = ((source >> 5) & 1) == ((target >> 5) & 1), source < target
    counts = counts_before([pair == g for g in range(4)], same, before)
    place = sum(jnp.where(pair == g, counts[g], 0) for g in range(4))
    pol = iota((8, 128), 1) & 1
    pairs, high, low = to_rows([pair, place >> 4, place & 15], h)
    notes[0] = pairs * K + pol * (K // 2) + high * 16 + low

    loads[2].wait()
    pl.semaphore_wait(barrier, PEERS - 1 + 7)

    def first(away, part, there, there_core, device):
        i = 2 * (1 - away) + part
        return pltpu.make_async_remote_copy(
            v.at[part, there, rem(h + away, 2), there_core], buf.at[i, me], send1.at[i], recv1.at[i],
            device_id=device, device_id_type=MESH,
        )

    def all_first(i):
        every = buf.at[i, pl.ds(0, PEERS - 1)]
        return pltpu.make_async_remote_copy(
            every, every, send1.at[i], recv1.at[i], device_id=group(jnp.int32(0), 0)[2], device_id_type=MESH
        )

    def chunks(act):
        for away in (1, 0):

            def step(part, carry, away=away):
                act(away, part)
                return carry

            lax.fori_loop(0, 2, step, 0)

    def start(away, part):
        others(lambda *peer: first(away, part, *peer).start())
        buf[2 * (1 - away) + part, me] = v[part, xy, rem(h + away, 2), core]

    chunks(start)

    tall = iota((K, 128), 0)

    def pick(g, carry):
        for b in range(8):
            hit = tall == notes[0, b : b + 1] - g * K
            select[g, :, b * 128 : (b + 1) * 128] = jnp.where(hit, 1.0, 0.0).astype(BF)
        return carry

    lax.fori_loop(0, 4, pick, 0)

    def second(away, part, o):
        i, row = 2 * (1 - away) + part, rem(t + o, 4)
        return pltpu.make_async_remote_copy(
            stage.at[i, row], recv.at[part, t, pl.ds(h * K, K)], send2.at[i], recv2.at[part, depth],
            device_id=column(rem(h + away, 2), row), device_id_type=MESH,
        )

    def pack(away, part):
        i = 2 * (1 - away) + part
        all_first(i).wait_recv()

        def one(o, carry):
            row = rem(t + o, 4)
            rows = buf[i].reshape(PEERS * 32, 128)
            stage[i, row] = jnp.dot(select[row], rows, preferred_element_type=jnp.float32).astype(BF)
            if away == 0:
                pl.when(o < 4)(lambda: second(away, part, o).start())
            else:
                second(away, part, o).start()
            return carry

        lax.fori_loop(1 - away, 5 - away, one, 0)
        if away == 0:
            recv[part, t, pl.ds(h * K, K)] = stage[i, t]

    chunks(pack)

    for i in range(4):
        all_first(i).wait_send()

    mine = [slot == 2 * t + s for s in range(2)]
    ranks = counts_before(mine, source >= 0, before)
    final = sum(jnp.where(mine[s], s * SLOT + 2 * ranks[s], 0) for s in range(2))
    for half in range(2):
        pairs, high, low, top, rest = to_rows([pair, place >> 4, place & 15, final >> 8, final & 255], half)
        notes[1 + 3 * half] = jnp.where(pairs == t, half * K + pol * (K // 2) + high * 16 + low, -1)
        notes[2 + 3 * half] = top
        notes[3 + 3 * half] = rest + pol
    sub = iota((8, 128), 0)
    taller = iota((2 * K, 128), 0)

    def find(b, found):
        one = pl.ds(b, 1)
        for n in (1, 4):
            hit = jnp.where(taller == notes[n, one], 1.0, 0.0).astype(BF)
            known = jnp.where(
                sub == 0, notes[n + 1, one], jnp.where(sub == 1, notes[n + 2, one], jnp.where(sub == 2, 1, 0))
            )
            found = found + lax.dot_general(as_bf16(known), hit, NT, preferred_element_type=jnp.float32)
        return found

    found = lax.fori_loop(0, 8, find, jnp.zeros((8, 2 * K), jnp.float32))
    at = jnp.where(found[2:3] > 0.5, 256.0 * found[0:1] + found[1:2], -1.0).astype(jnp.int32)
    for b in range(6):
        hit = iota((128, 2 * K), 0) == at - b * 128
        merge[b] = jnp.where(hit, 1.0, 0.0).astype(BF)

    def arrived(part, half, row):
        pltpu.make_async_remote_copy(
            stage.at[0, 0], recv.at[part, row, pl.ds(half * K, K)], send2.at[0], recv2.at[part, half * 4 + row],
            device_id=column(half, row), device_id_type=MESH,
        ).wait_recv()

    def finish(n, carry):
        part, row = div(n, 4), rem(t + n, 4)
        arrived(part, 1 - h, row)
        pl.when(rem(n, 4) != 0)(lambda: arrived(part, h, row))
        for b in range(6):
            z[part, row, b * 128 : (b + 1) * 128] = jnp.dot(
                merge[b], recv[part, row], preferred_element_type=jnp.float32
            ).astype(BF)
        return carry

    lax.fori_loop(0, 8, finish, 0)

    def sent(away, part):
        i = 2 * (1 - away) + part
        every = stage.at[i, pl.ds(0, 3 + away)]
        pltpu.make_async_remote_copy(
            every, every, send2.at[i], recv2.at[0, 0], device_id=column(h, rem(t + 1, 4)), device_id_type=MESH
        ).wait_send()

    chunks(sent)


def correlator(number, K):
    def call(voltages, assigned, index):
        return pl.pallas_call(
            functools.partial(correlate, K),
            out_shape=jax.ShapeDtypeStruct((2, 4, 2 * SLOT, 128), BF),
            in_specs=[ANY, ANY, ANY],
            out_specs=VMEM,
            scratch_shapes=[
                pltpu.VMEM((8, 128), jnp.int32),
                pltpu.SMEM((8,), jnp.int32),
                pltpu.VMEM((2, 16, 2, 2, 32, 128), BF),
                pltpu.VMEM((4, PEERS, 32, 128), BF),
                pltpu.VMEM((4, K, 1024), BF),
                pltpu.VMEM((6, 128, 2 * K), BF),
                pltpu.VMEM((4, 4, K, 128), BF),
                pltpu.VMEM((2, 4, 2 * K, 128), BF),
                pltpu.VMEM((7, 8, 128), jnp.int32),
                pltpu.SemaphoreType.DMA((3,)),
                pltpu.SemaphoreType.DMA((4,)),
                pltpu.SemaphoreType.DMA((4,)),
                pltpu.SemaphoreType.DMA((4,)),
                pltpu.SemaphoreType.DMA((2, 8)),
            ],
            compiler_params=pltpu.CompilerParams(
                collective_id=number, has_side_effects=True, vmem_limit_bytes=48 << 20
            ),
            name=f"gather_{K}",
        )(assigned, index, voltages)

    return call


def gram_kernel(z_ref, out_ref, result, sem):
    def samples(part, s):
        rows = slice(s * SLOT, (s + 1) * SLOT)
        return jnp.concatenate([z_ref[part, b, rows] for b in range(4)], axis=1)

    def times(a, b):
        return lax.dot_general(a, b, NT, preferred_element_type=jnp.float32)

    stores = []
    for s in range(2):
        re, im = samples(0, s), samples(1, s)
        for k in range(2):
            if k == 0:
                both = jnp.concatenate([re, im], axis=1)
                result[s, k] = times(both, both)
            else:
                cross = times(im, re)
                result[s, k] = cross - cross.T
            store = pltpu.make_async_copy(result.at[s, k], out_ref.at[s, 0, k], sem.at[s, k])
            store.start()
            stores.append(store)
    for store in stores:
        store.wait()


def gram(z):
    return pl.pallas_call(
        gram_kernel,
        out_shape=jax.ShapeDtypeStruct((2, 1, 2, SLOT, SLOT), jnp.float32),
        in_specs=[VMEM],
        out_specs=pl.BlockSpec(memory_space=pltpu.HBM),
        scratch_shapes=[pltpu.VMEM((2, 2, SLOT, SLOT), jnp.float32), pltpu.SemaphoreType.DMA((2, 2))],
        name="gram",
    )(z)


def shards(voltages, assignment, slot_subarray_index):
    assigned = assignment.reshape(8, 128)
    level = pl.pallas_call(
        level_kernel,
        out_shape=jax.ShapeDtypeStruct((1,), jnp.int32),
        in_specs=[VMEM, SMEM],
        out_specs=SMEM,
        name="level",
    )(assigned, slot_subarray_index)
    branches = [correlator(number, K) for number, K in enumerate(LEVELS)]
    voltages = voltages.reshape(2, 16, 2, 2, 32, 128)
    return gram(lax.switch(level[0], branches, voltages, assigned, slot_subarray_index))


def solution(mesh):
    placed = (P(None, None, "chan", "tm"), P(), P())
    return jax.shard_map(
        shards,
        mesh=mesh,
        in_specs=placed,
        out_specs=P("tm", "chan", None, None, None),
        check_vma=False,
    )
```

profile of v0, /device:TPU:1, one launch (start us, length us, event | category | flops | bytes accessed | tf_op | source)
XLA Modules:
  0.0 61.1 jit_solution(13351542419500904692)
XLA Ops:
  0.0 1.5 %level.1 = s32[1]{0:T(128)} custom-call(s32[8,128]{1,0:T(8,128)} %bitcast.13, s32[8]{0:T(128)} %index_ref.1), custom_call_target="tpu_custom_call" | custom-call | tf_op jit(solution)/shard_map/level/pallas_call | solution.py:329
  2.1 56.5 %conditional.1 = (bf16[2,4,768,128]{3,2,1,0:T(8,128)(2,1)S(1)}) conditional(s32[]{:T(128)} %bitcast.1, (s32[8,128]{1,0:T(8,128)}, s32[8]{0:T(128)}, bf16[2,16,2,2,32,128]{5,4,3,2,1,0:T(8,128)(2,1)}) %tuple.56, (s32[8,128]{1,0:T(8,128)}, s32[8]{0:T(128)}, bf16[2,16,2,2,32,128]{5,4,3,2,1,0:T(8,128)(2,1)}) %tuple.57, ...), branch_computations={%region_0.0_spmd, %region_1.0_spmd, %region_2.0_spmd, %region_3.0_... | conditional | bytes 8 | solution.py:338
  2.3 56.0 %gather_400.1 = bf16[2,4,768,128]{3,2,1,0:T(8,128)(2,1)S(1)} custom-call(s32[8,128]{1,0:T(8,128)} %get-tuple-element.97.assigned_hbm, s32[8]{0:T(128)} %get-tuple-element.98.index_hbm, bf16[2,16,2,2,32,128]{5,4,3,2,1,0:T(8,128)(2,1)} %get-tuple-element.99.v_ref), custom_call_target="tpu_custom_call" | custom-call | tf_op jit(solution)/shard_map/cond/branch_7_fun/gather_400/pallas_call | solution.py:261
  58.6 2.4 %gram.1 = f32[2,1,2,384,384]{4,3,2,1,0:T(8,128)} custom-call(bf16[2,4,768,128]{3,2,1,0:T(8,128)(2,1)S(1)} %get-tuple-element.106.z_ref), custom_call_target="tpu_custom_call" | custom-call | tf_op jit(solution)/shard_map/gram/pallas_call | solution.py:317
where the time goes:
time: 61.3 us; the launch traced here: 61.1 us
  Pallas kernels  59.9 us (98%)
  between operations  0.85 us (1%)
    pallas_call x1, Pallas kernels, call(): pl.pallas_call(functools.partial(correlate, K), out_shape=jax.ShapeDtypeS...  56 us
    pallas_call x1, Pallas kernels, gram(): pl.pallas_call(gram_kernel, out_shape=jax.ShapeDtypeStruct((2, 1, 2, SLOT...  2.36 us
    pallas_call x1, Pallas kernels, shards(): pl.pallas_call(level_kernel, out_shape=jax.ShapeDtypeStruct((1,), jnp.int...  1.47 us

commit v1 on v0

--- a/solution.py
+++ b/solution.py
@@ -226,7 +226,7 @@
     at = jnp.where(found[2:3] > 0.5, 256.0 * found[0:1] + found[1:2], -1.0).astype(jnp.int32)
     for b in range(6):
         hit = iota((128, 2 * K), 0) == at - b * 128
-        merge[b] = jnp.where(hit, 1.0, 0.0).astype(BF)
+        merge[b * 128 : (b + 1) * 128] = jnp.where(hit, 1.0, 0.0).astype(BF)
 
     def arrived(part, half, row):
         pltpu.make_async_remote_copy(
@@ -235,16 +235,21 @@
         ).wait_recv()
 
     def finish(n, carry):
-        part, row = div(n, 4), rem(t + n, 4)
-        arrived(part, 1 - h, row)
-        pl.when(rem(n, 4) != 0)(lambda: arrived(part, h, row))
-        for b in range(6):
-            z[part, row, b * 128 : (b + 1) * 128] = jnp.dot(
-                merge[b], recv[part, row], preferred_element_type=jnp.float32
-            ).astype(BF)
+        part, pair = div(n, 2), 2 * rem(n, 2)
+        blocks = [rem(t + pair + o, 4) for o in range(2)]
+        for o in range(2):
+            arrived(part, 1 - h, blocks[o])
+            if o == 0:
+                pl.when(pair != 0)(lambda: arrived(part, h, blocks[0]))
+            else:
+                arrived(part, h, blocks[1])
+        both = jnp.concatenate([recv[part, block] for block in blocks], axis=1)
+        placed = jnp.dot(merge[...], both, preferred_element_type=jnp.float32).astype(BF)
+        for o in range(2):
+            z[part, blocks[o]] = placed[:, o * 128 : (o + 1) * 128]
         return carry
 
-    lax.fori_loop(0, 8, finish, 0)
+    lax.fori_loop(0, 4, finish, 0)
 
     def sent(away, part):
         i = 2 * (1 - away) + part
@@ -269,7 +274,7 @@
                 pltpu.VMEM((2, 16, 2, 2, 32, 128), BF),
                 pltpu.VMEM((4, PEERS, 32, 128), BF),
                 pltpu.VMEM((4, K, 1024), BF),
-                pltpu.VMEM((6, 128, 2 * K), BF),
+                pltpu.VMEM((2 * SLOT, 2 * K), BF),
                 pltpu.VMEM((4, 4, K, 128), BF),
                 pltpu.VMEM((2, 4, 2 * K, 128), BF),
                 pltpu.VMEM((7, 8, 128), jnp.int32),

time: 61.3 us -> 54.9 us (0.90)
  Pallas kernels: 59.9 us -> 53.6 us
    pallas_call x1, Pallas kernels: 56 us -> 49.8 us  [call(): pl.pallas_call(functools.partial(correlate, K), out_shape=jax.ShapeDtypeS...]
where the time goes in v1:
time: 54.9 us; the launch traced here: 54.8 us
  Pallas kernels  53.6 us (98%)
  between operations  0.87 us (2%)
    pallas_call x1, Pallas kernels, call(): pl.pallas_call(functools.partial(correlate, K), out_shape=jax.ShapeDtypeS...  49.8 us
    pallas_call x1, Pallas kernels, gram(): pl.pallas_call(gram_kernel, out_shape=jax.ShapeDtypeStruct((2, 1, 2, SLOT...  2.36 us
    pallas_call x1, Pallas kernels, shards(): pl.pallas_call(level_kernel, out_shape=jax.ShapeDtypeStruct((1,), jnp.int...  1.47 us

profile of v1, /device:TPU:1, one launch (start us, length us, event | category | flops | bytes accessed | tf_op | source)
XLA Modules:
  0.0 54.8 jit_solution(9007549640648144734)
XLA Ops:
  0.0 1.5 %level.1 = s32[1]{0:T(128)} custom-call(s32[8,128]{1,0:T(8,128)} %bitcast.13, s32[8]{0:T(128)} %index_ref.1), custom_call_target="tpu_custom_call" | custom-call | tf_op jit(solution)/shard_map/level/pallas_call | solution.py:334
  2.1 50.1 %conditional.1 = (bf16[2,4,768,128]{3,2,1,0:T(8,128)(2,1)S(1)}) conditional(s32[]{:T(128)} %bitcast.1, (s32[8,128]{1,0:T(8,128)}, s32[8]{0:T(128)}, bf16[2,16,2,2,32,128]{5,4,3,2,1,0:T(8,128)(2,1)}) %tuple.56, (s32[8,128]{1,0:T(8,128)}, s32[8]{0:T(128)}, bf16[2,16,2,2,32,128]{5,4,3,2,1,0:T(8,128)(2,1)}) %tuple.57, ...), branch_computations={%region_0.0_spmd, %region_1.0_spmd, %region_2.0_spmd, %region_3.0_... | conditional | bytes 8 | solution.py:343
  2.2 49.8 %gather_336.1 = bf16[2,4,768,128]{3,2,1,0:T(8,128)(2,1)S(1)} custom-call(s32[8,128]{1,0:T(8,128)} %get-tuple-element.85.assigned_hbm, s32[8]{0:T(128)} %get-tuple-element.86.index_hbm, bf16[2,16,2,2,32,128]{5,4,3,2,1,0:T(8,128)(2,1)} %get-tuple-element.87.v_ref), custom_call_target="tpu_custom_call" | custom-call | tf_op jit(solution)/shard_map/cond/branch_3_fun/gather_336/pallas_call | solution.py:266
  52.2 2.4 %gram.1 = f32[2,1,2,384,384]{4,3,2,1,0:T(8,128)} custom-call(bf16[2,4,768,128]{3,2,1,0:T(8,128)(2,1)S(1)} %get-tuple-element.106.z_ref), custom_call_target="tpu_custom_call" | custom-call | tf_op jit(solution)/shard_map/gram/pallas_call | solution.py:322

commit v2 on v1

--- a/solution.py
+++ b/solution.py
@@ -85,7 +85,9 @@
     x, y = div(xy, 4), rem(xy, 4)
 
     def group(four, i):
-        there = rem(x + 3 - div(four, 2), 4) * 4 + rem(y + 3 - 2 * rem(four, 2) - i // 2, 4)
+        a, q, s = div(four, 2), rem(four, 2), i // 2
+        dx, dy = 2 + a + div(a * (a - 1), 2), 2 + s - q * (1 + 2 * s)
+        there = rem(x + dx, 4) * 4 + rem(y + dy, 4)
         there_core = rem(core + 1 - i % 2, 2)
         return there, there_core, {"chan": (there * 2 + h) * 2 + there_core, "tm": t}
 

time: 54.9 us -> 58.8 us (1.071); the launches traced: 54.8 us -> 59.4 us
  Pallas kernels: 53.6 us -> 57.8 us
    pallas_call x1, Pallas kernels: 49.8 us -> 54 us  [call(): pl.pallas_call(functools.partial(correlate, K), out_shape=jax.ShapeDtypeS...]
where the time goes in v2:
time: 58.8 us; the launch traced here: 59.4 us
  Pallas kernels  57.8 us (98%)
  between operations  0.87 us (1%)
  loops' own time  0.71 us (1%)
    pallas_call x1, Pallas kernels, call(): pl.pallas_call(functools.partial(correlate, K), out_shape=jax.ShapeDtypeS...  54 us
    pallas_call x1, Pallas kernels, gram(): pl.pallas_call(gram_kernel, out_shape=jax.ShapeDtypeStruct((2, 1, 2, SLOT...  2.36 us
    pallas_call x1, Pallas kernels, shards(): pl.pallas_call(level_kernel, out_shape=jax.ShapeDtypeStruct((1,), jnp.int...  1.47 us

profile of v2, /device:TPU:1, one launch (start us, length us, event | category | flops | bytes accessed | tf_op | source)
XLA Modules:
  0.0 59.4 jit_solution(15412858014745918899)
XLA Ops:
  0.0 1.5 %level.1 = s32[1]{0:T(128)} custom-call(s32[8,128]{1,0:T(8,128)} %bitcast.13, s32[8]{0:T(128)} %index_ref.1), custom_call_target="tpu_custom_call" | custom-call | tf_op jit(solution)/shard_map/level/pallas_call | solution.py:336
  2.1 54.7 %conditional.1 = (bf16[2,4,768,128]{3,2,1,0:T(8,128)(2,1)S(1)}) conditional(s32[]{:T(128)} %bitcast.1, (s32[8,128]{1,0:T(8,128)}, s32[8]{0:T(128)}, bf16[2,16,2,2,32,128]{5,4,3,2,1,0:T(8,128)(2,1)}) %tuple.56, (s32[8,128]{1,0:T(8,128)}, s32[8]{0:T(128)}, bf16[2,16,2,2,32,128]{5,4,3,2,1,0:T(8,128)(2,1)}) %tuple.57, ...), branch_computations={%region_0.0_spmd, %region_1.0_spmd, %region_2.0_spmd, %region_3.0_... | conditional | bytes 8 | solution.py:345
  2.3 54.0 %gather_384.1 = bf16[2,4,768,128]{3,2,1,0:T(8,128)(2,1)S(1)} custom-call(s32[8,128]{1,0:T(8,128)} %get-tuple-element.94.assigned_hbm, s32[8]{0:T(128)} %get-tuple-element.95.index_hbm, bf16[2,16,2,2,32,128]{5,4,3,2,1,0:T(8,128)(2,1)} %get-tuple-element.96.v_ref), custom_call_target="tpu_custom_call" | custom-call | tf_op jit(solution)/shard_map/cond/branch_6_fun/gather_384/pallas_call | solution.py:268
  56.8 2.4 %gram.1 = f32[2,1,2,384,384]{4,3,2,1,0:T(8,128)} custom-call(bf16[2,4,768,128]{3,2,1,0:T(8,128)(2,1)S(1)} %get-tuple-element.106.z_ref), custom_call_target="tpu_custom_call" | custom-call | tf_op jit(solution)/shard_map/gram/pallas_call | solution.py:324
